TPU v7x, 32 devices: a whole 2x2x4 slice. The times are simulated.
32 devices in a mesh: dom: 4 (over x, core), grp: 8 (over z, y).
Axes of the slice: x: 2, y: 2, z: 4, core: 2. Of those that a mesh axis runs over, the one named last changes fastest.
Arguments:
- features: bfloat16 [131072, 256], P(('dom', 'grp')), may hold values from -6 to 6
- w_fine: bfloat16 [256, 256], replicated, may hold values from -0.375 to 0.375
- adj_tiles: bfloat16 [1024, 20, 128, 128], P(('dom', 'grp')), may hold values from -0.125 to 0.125
- tile_cols: int32 [1024, 20], P(('dom', 'grp')), may hold values from 0 to 39
- tile_count: int32 [1024], P(('dom', 'grp')), may hold values from 1 to 20, as said below
- send_lower: int32 [128], P(('dom', 'grp')), may hold values from 0 to 31
- send_upper: int32 [128], P(('dom', 'grp')), may hold values from 0 to 31
- assign: int32 [131072], P(('dom', 'grp')), may hold values from 0 to 1023, as said below
- w_coarse: bfloat16 [256, 256], replicated, may hold values from -0.375 to 0.375
- coarse_adj: bfloat16 [1024, 1024], P(('dom', 'grp')), may hold values from -0.1875 to 0.1875
Outputs:
- output: bfloat16 [131072, 256], P(('dom', 'grp'))
Inputs may be any that keep to these rules, and one draw needn't show every extreme that they name: The first tile_count[r] slots of block row r are live; the others are ignored. `assign`: every coarse node is the coarse node of at least one vertex.
All inputs are finite; a program needn't handle non-finite values.
Results may differ from a plain program's by a relative error of at most 0.011.
Values may be sent and summed in bfloat16 or wider, within the bound.
No kernel may reach another device: no remote copies, remote signals or barrier semaphores. Data moves between devices by JAX's collectives and lax.ppermute only.
A program may use at most 192 MiB of HBM per device.

v0:
```python
import functools

import jax
import jax.numpy as jnp
from jax import lax
from jax.experimental import pallas as pl
from jax.experimental.pallas import tpu as pltpu
from jax.sharding import PartitionSpec as P


AXES = ("dom", "grp")
F32, BF16, I32 = jnp.float32, jnp.bfloat16, jnp.int32
LANES = 128
EXTRA = 16
PACK = 16
I16 = jnp.int16


def bits_of(count):
    assert count & (count - 1) == 0
    return [1 << i for i in range(count.bit_length() - 1)]


def dot(a, b):
    return jnp.dot(a, b, preferred_element_type=F32)


def cost(flops, nbytes):
    return pl.CostEstimate(flops=int(flops), bytes_accessed=int(nbytes), transcendentals=0)


VMEM = pl.BlockSpec(memory_space=pltpu.VMEM)
SMEM = pl.BlockSpec(memory_space=pltpu.SMEM)
ANY = pl.BlockSpec(memory_space=pltpu.HBM)


def one_hot(packed, rows, first):
    width = packed.shape[1]
    sub = lax.broadcasted_iota(I32, (PACK, width), 0)
    out = []
    for at in range(0, rows, PACK):
        hot = packed == (sub + (first + at)).astype(I16)
        out.append(jnp.where(hot, jnp.ones((), BF16), jnp.zeros((), BF16)))
    return jnp.concatenate(out, axis=0)


def in_hbm(x):
    return pltpu.with_memory_space_constraint(x, pltpu.HBM)


def sums_kernel(
    assign_hbm, x_hbm, keep_ref, send_ref, x_ref, assign_ref, acc, cnt, tail, sems, *, slots, rows, base, digits, width
):
    dom = lax.axis_index("dom")
    chunks = x_ref.shape[0] // width

    def fetch(i):
        at = pl.ds(i * width, width)
        return pltpu.make_async_copy(x_hbm.at[at, :], x_ref.at[at, :], sems.at[i])

    ids = pltpu.make_async_copy(assign_hbm, assign_ref, sems.at[chunks])
    ids.start()
    for i in range(chunks):
        fetch(i).start()
    ids.wait()
    for i in range(chunks):
        nodes = assign_ref[:, i * width : (i + 1) * width]
        packed = jnp.broadcast_to(nodes, (PACK, width)).astype(I16)
        high = lax.broadcasted_iota(I32, (cnt.shape[0], width), 0) == lax.shift_right_logical(nodes, 7)
        low = lax.broadcasted_iota(I32, (LANES, width), 0) == (nodes & (LANES - 1))
        count = lax.dot_general(
            jnp.where(high, 1.0, 0.0).astype(BF16),
            jnp.where(low, 1.0, 0.0).astype(BF16),
            (((1,), (1,)), ((), ())),
            preferred_element_type=F32,
        )
        cnt[...] = count if i == 0 else cnt[...] + count
        fetch(i).wait()
        x = x_ref[i * width : (i + 1) * width, :]
        for p, s in enumerate(slots):
            part = dot(one_hot(packed, rows, (dom ^ s) * rows), x)
            acc[p] = part if i == 0 else acc[p] + part
    per = rows // LANES
    half = len(slots) // 2
    for p, s in enumerate(slots):
        tail[...] = jnp.zeros_like(tail)
        for h in range(per):
            c = cnt[pl.ds((dom ^ s) * per + h, 1), :]
            over = [c] + [jnp.floor((c + 0.5) * (1.0 / base**d)) for d in range(1, digits)]
            for d in range(digits):
                digit = over[d] if d == digits - 1 else over[d] - base * over[d + 1]
                tail[d * per + h : d * per + h + 1, 0:LANES] = digit
        out = keep_ref if p < half else send_ref
        at = (p % half) * (rows + EXTRA)
        out[at : at + rows, :] = acc[p].astype(out.dtype)
        out[at + rows : at + rows + EXTRA, :] = tail[...].astype(out.dtype)


def segment_sums(features, assign, slots, rows, base, digits):
    verts, feat = features.shape
    width = min(verts, 1024)
    half = len(slots) // 2
    shape = (half * (rows + EXTRA), feat)
    nodes = len(slots) * rows
    return pl.pallas_call(
        functools.partial(sums_kernel, slots=slots, rows=rows, base=base, digits=digits, width=width),
        out_shape=(
            jax.ShapeDtypeStruct(shape, F32),
            jax.ShapeDtypeStruct(shape, BF16),
            jax.ShapeDtypeStruct((verts, feat), BF16),
        ),
        in_specs=[ANY, ANY],
        out_specs=(VMEM, VMEM, VMEM),
        scratch_shapes=[
            pltpu.VMEM((1, verts), I32),
            pltpu.VMEM((len(slots), rows, feat), F32),
            pltpu.VMEM((max(16, nodes // LANES), LANES), F32),
            pltpu.VMEM((EXTRA, feat), F32),
            pltpu.SemaphoreType.DMA((verts // width + 1,)),
        ],
        compiler_params=pltpu.CompilerParams(vmem_limit_bytes=16 << 20),
        cost_estimate=cost(2 * nodes * verts * feat, verts * feat * 2),
        name="sums",
    )(in_hbm(assign.reshape(1, verts)), in_hbm(features))


def coarse_kernel(keep_ref, recv_ref, w_ref, out_ref, tail, *, rows, base, digits):
    per = rows // LANES
    feat = keep_ref.shape[1]
    tail[...] = keep_ref[rows:, :] + recv_ref[rows:, :].astype(F32)
    done = []
    for h in range(per):
        c = tail[h : h + 1, 0:LANES]
        for d in range(1, digits):
            c = c + tail[d * per + h : d * per + h + 1, 0:LANES] * float(base**d)
        root = jnp.sqrt(jnp.broadcast_to(c, (LANES, LANES)).T)
        at = slice(h * LANES, (h + 1) * LANES)
        total = keep_ref[at, :] + recv_ref[at, :].astype(F32)
        done.append(
            jnp.concatenate(
                [total[:, j : j + LANES] / root for j in range(0, feat, LANES)], axis=1
            ).astype(BF16)
        )
    out_ref[...] = dot(jnp.concatenate(done, axis=0), w_ref[...]).astype(BF16)


def coarse_part(keep, recv, w, rows, base, digits):
    feat = keep.shape[1]
    return pl.pallas_call(
        functools.partial(coarse_kernel, rows=rows, base=base, digits=digits),
        out_shape=jax.ShapeDtypeStruct((rows, feat), BF16),
        in_specs=[VMEM, VMEM, VMEM],
        out_specs=VMEM,
        scratch_shapes=[pltpu.VMEM((EXTRA, feat), F32)],
        compiler_params=pltpu.CompilerParams(vmem_limit_bytes=8 << 20),
        cost_estimate=cost(2 * rows * feat * feat, rows * feat * 8),
        name="coarse",
    )(keep, recv, w)


def mix_kernel(*refs, slots, rows, own, order):
    pa_ref, pb_ref, *pieces, out_ref, proj, wide, own_rows = refs
    dom = lax.axis_index("dom")
    me = dom * lax.axis_size("grp") + lax.axis_index("grp")
    half = len(slots) // 2
    for p, s in enumerate(slots):
        src = pa_ref if p < half else pb_ref
        value = src[(p % half) * rows : (p % half + 1) * rows, :]
        at = pl.multiple_of((dom ^ s) * rows, rows)
        proj[pl.ds(at, rows), :] = value
        wide[pl.ds(at, rows), :] = value.astype(F32)
    for q, t in enumerate(order):
        at = pl.multiple_of((me ^ t) * own, own)
        own_rows[q * own : (q + 1) * own, :] = wide[pl.ds(at, own), :]
    adj = jnp.concatenate([piece[...].astype(F32) for piece in pieces], axis=0).astype(BF16)
    out_ref[...] = (own_rows[...] + dot(adj, proj[...])).astype(BF16)


def mixed_rows(pa, pb, pieces, slots, rows, own, order):
    nodes, feat = len(slots) * rows, pa.shape[1]
    got = len(order) * own
    return pl.pallas_call(
        functools.partial(mix_kernel, slots=slots, rows=rows, own=own, order=order),
        out_shape=jax.ShapeDtypeStruct((got, feat), BF16),
        in_specs=[VMEM] * (2 + len(pieces)),
        out_specs=VMEM,
        scratch_shapes=[
            pltpu.VMEM((nodes, feat), BF16),
            pltpu.VMEM((nodes, feat), F32),
            pltpu.VMEM((got, feat), F32),
        ],
        compiler_params=pltpu.CompilerParams(vmem_limit_bytes=12 << 20),
        cost_estimate=cost(2 * got * nodes * feat, got * nodes * 2),
        name="mix",
    )(pa, pb, *pieces)


def join_kernel(a_ref, b_ref, out_ref):
    rows = a_ref.shape[0]
    out_ref[0:rows, :] = a_ref[...]
    out_ref[rows:, :] = b_ref[...]


def join(a, b):
    shape = (a.shape[0] + b.shape[0], a.shape[1])
    return pl.pallas_call(
        join_kernel,
        out_shape=jax.ShapeDtypeStruct(shape, a.dtype),
        in_specs=[VMEM, VMEM],
        out_specs=VMEM,
        compiler_params=pltpu.CompilerParams(vmem_limit_bytes=4 << 20),
        cost_estimate=cost(shape[0] * shape[1], shape[0] * shape[1] * 4),
        name="join",
    )(a, b)


def proj_kernel(low_idx, up_idx, x_ref, w_ref, own_ref, low_ref, up_ref, *, width):
    chunks = x_ref.shape[0] // width
    block = low_ref.shape[1]
    w = w_ref[...]
    for i in range(chunks):
        done = dot(x_ref[i * width : (i + 1) * width, :], w).astype(BF16)
        own_ref[i * (width // block) : (i + 1) * (width // block)] = done.reshape(width // block, block, done.shape[1])
    for h in range(low_ref.shape[0]):
        low_ref[h] = own_ref[low_idx[h]]
        up_ref[h] = own_ref[up_idx[h]]


def projection(send_lower, send_upper, features, w, block):
    verts, feat = features.shape
    halo = send_lower.shape[0]
    sent = jax.ShapeDtypeStruct((halo, block, feat), BF16)
    return pl.pallas_call(
        functools.partial(proj_kernel, width=min(verts, 1024)),
        out_shape=(jax.ShapeDtypeStruct((verts // block, block, feat), BF16), sent, sent),
        in_specs=[SMEM, SMEM, VMEM, VMEM],
        out_specs=(VMEM, VMEM, VMEM),
        compiler_params=pltpu.CompilerParams(vmem_limit_bytes=14 << 20),
        cost_estimate=cost(2 * verts * feat * feat, 4 * verts * feat),
        name="proj",
    )(send_lower, send_upper, features, w)


GROUP = 4
TURNS = 3
LAG = 2


def fine_kernel(cols_ref, live_ref, own_ref, below_ref, above_ref, adj_hbm, out_ref, ext, tiles, sems):
    rows, block = own_ref.shape[0], own_ref.shape[1]
    halo = below_ref.shape[0]

    def groups(r):
        return lax.div(live_ref[r] + (GROUP - 1), GROUP)

    def fetch(r, i):
        at = pl.ds(i * GROUP, GROUP)
        return pltpu.make_async_copy(adj_hbm.at[r, at], tiles.at[r, at], sems.at[r, i])

    @pl.loop(0, rows)
    def _(r):
        @pl.loop(0, groups(r))
        def _(i):
            fetch(r, i).start()

    ext[0:rows] = own_ref[...]
    ext[rows : rows + halo] = below_ref[...]
    ext[rows + halo :] = above_ref[...]

    def body(*accs):
        def push(columns):
            for q in range(2):
                rhs = jnp.concatenate([ext[c] for c in columns[2 * q : 2 * q + 2]], axis=0)
                pltpu.matmul_push_rhs(rhs, staging_register=0, mxu_index=q)

        def columns_of(r, i):
            return [cols_ref[i * GROUP + j, r] for j in range(GROUP)]

        def finish(r, turn):
            at = pl.ds(pl.multiple_of(r * block, block), block)
            out_ref[at, :] = pltpu.matmul_pop(accs[turn]) + pltpu.matmul_pop(accs[TURNS + turn])

        def row(r, turn, before):
            live = live_ref[r]
            following = jnp.minimum(r + 1, rows - 1)

            def with_groups(count):
                def run():
                    for i in range(count):
                        fetch(r, i).wait()
                    for i in range(count):
                        coming = columns_of(following, 0) if i + 1 == count else columns_of(r, i + 1)
                        for q in range(2):
                            lhs = []
                            for j in range(2):
                                k = i * GROUP + 2 * q + j
                                tile = tiles[r, k]
                                if i + 1 == count and 2 * q + j > 0:
                                    tile = jnp.where(k < live, tile, jnp.zeros_like(tile))
                                lhs.append(tile)
                            lhs = jnp.concatenate(lhs, axis=1)
                            pltpu.matmul_acc_lhs(accs[q * TURNS + turn], lhs, load_staged_rhs=0)
                        push(coming)
                        if i == 0 and before is not None:
                            finish(before, (turn + TURNS - LAG) % TURNS)

                return run

            lax.switch(groups(r) - 1, [with_groups(n + 1) for n in range(cols_ref.shape[0] // GROUP)])

        push(columns_of(0, 0))
        for r in range(LAG):
            row(r, r % TURNS, None)

        @pl.loop(0, (rows - LAG) // TURNS)
        def _(h):
            for turn in range(TURNS):
                r = h * TURNS + turn + LAG
                row(r, (turn + LAG) % TURNS, r - LAG)

        for r in range((rows - LAG) // TURNS * TURNS + LAG, rows):
            row(r, r % TURNS, r - LAG)
        spare = rows % TURNS
        for q in range(2):
            zero = jnp.zeros((block, 2 * block), BF16)
            pltpu.matmul_acc_lhs(accs[q * TURNS + spare], zero, load_staged_rhs=0)
        for r in range(rows - LAG, rows):
            finish(r, r % TURNS)
        for q in range(2):
            ext[0, 0:16, :] = pltpu.matmul_pop(accs[q * TURNS + spare])[0:16].astype(BF16)

    shape = (block, 2 * block)
    pl.run_scoped(body, *[pltpu.ACC(q)(shape, F32) for q in range(2) for _ in range(TURNS)])


def fine_rows(tile_cols, tile_count, own, below, above, adj_tiles):
    rows, slots, block, _ = adj_tiles.shape
    feat = own.shape[2]
    halo = below.shape[0]
    assert slots % GROUP == 0 and rows % 2 == 0 and feat == 2 * block
    return pl.pallas_call(
        fine_kernel,
        out_shape=jax.ShapeDtypeStruct((rows * block, feat), F32),
        in_specs=[SMEM, SMEM, VMEM, VMEM, VMEM, ANY],
        out_specs=VMEM,
        scratch_shapes=[
            pltpu.VMEM((rows + 2 * halo, block, feat), BF16),
            pltpu.VMEM((rows, slots, block, block), BF16),
            pltpu.SemaphoreType.DMA((rows, slots // GROUP)),
        ],
        compiler_params=pltpu.CompilerParams(vmem_limit_bytes=36 << 20),
        cost_estimate=cost(2 * rows * slots * block * block * feat, rows * slots * block * block * 2),
        name="fine",
    )(tile_cols.T, tile_count, own, below, above, in_hbm(adj_tiles))


def picked_rows(columns, m_ref, first):
    nodes = m_ref.shape[0]
    lane = (lax.broadcasted_iota(I32, (LANES, nodes), 1) + first).astype(I16)
    hots = []
    for column in columns:
        hot = jnp.concatenate([column] * (nodes // LANES), axis=1) == lane
        hots.append(jnp.where(hot, jnp.ones((), BF16), jnp.zeros((), BF16)))
    return dot(jnp.concatenate(hots, axis=0), m_ref[...])


def place_kernel(assign_ref, m_ref, fine_ref, out_ref, place_ref, *, own, gather_bits, width):
    me = lax.axis_index("dom") * lax.axis_size("grp") + lax.axis_index("grp")
    shift = own.bit_length() - 1
    assign = assign_ref[...]
    apart = lax.shift_right_logical(assign, shift) ^ me
    place = assign & (own - 1)
    for j, bit in enumerate(gather_bits):
        place = place + jnp.where((apart & bit) != 0, own << j, 0)
    place = place.astype(F32)
    for i in range(0, out_ref.shape[0], width):
        columns = []
        for j in range(i // LANES, (i + width) // LANES):
            column = jnp.broadcast_to(place[j : j + 1, :], (LANES, LANES)).T.astype(I32).astype(I16)
            place_ref[j * LANES : (j + 1) * LANES, :] = column
            columns.append(column)
        out_ref[i : i + width, :] = fine_ref[i : i + width, :] + picked_rows(columns, m_ref, 0)


def stored_columns(place_ref, start, width):
    return [place_ref[j : j + LANES, :] for j in range(start, start + width, LANES)]


def gain_kernel(place_ref, m_ref, fine_ref, out_ref, *, first, width):
    for i in range(0, out_ref.shape[0], width):
        columns = stored_columns(place_ref, i, width)
        out_ref[i : i + width, :] = fine_ref[i : i + width, :] + picked_rows(columns, m_ref, first)


def out_kernel(place_ref, m_ref, fine_ref, out_hbm, out_ref, sems, *, first, width):
    chunks = out_ref.shape[0] // width

    def store(i):
        at = pl.ds(i * width, width)
        return pltpu.make_async_copy(out_ref.at[at, :], out_hbm.at[at, :], sems.at[i])

    for i in range(chunks):
        at = slice(i * width, (i + 1) * width)
        picked = picked_rows(stored_columns(place_ref, i * width, width), m_ref, first)
        out_ref[at, :] = jnp.maximum(fine_ref[at, :] + picked, 0.0).astype(BF16)
        store(i).start()
    for i in range(chunks):
        store(i).wait()


def output_rows(assign, part_of, count, fine, own, gather_bits):
    verts, feat = fine.shape
    width = min(verts, 1024)
    place, first = None, 0
    for step in range(count):
        m = part_of(step)
        nodes = m.shape[0]
        shared = dict(
            compiler_params=pltpu.CompilerParams(vmem_limit_bytes=16 << 20),
            cost_estimate=cost(2 * verts * nodes * feat, verts * feat * 6),
        )
        wide = jax.ShapeDtypeStruct((verts, feat), F32)
        if step == 0:
            fine, place = pl.pallas_call(
                functools.partial(place_kernel, own=own, gather_bits=gather_bits, width=width),
                out_shape=(wide, jax.ShapeDtypeStruct((verts, LANES), I16)),
                in_specs=[VMEM] * 3,
                out_specs=(VMEM, VMEM),
                name="place",
                **shared,
            )(assign.reshape(verts // LANES, LANES), m, fine)
        elif step + 1 < count:
            fine = pl.pallas_call(
                functools.partial(gain_kernel, first=first, width=width),
                out_shape=wide,
                in_specs=[VMEM] * 3,
                out_specs=VMEM,
                name="gain",
                **shared,
            )(place, m, fine)
        else:
            return pl.pallas_call(
                functools.partial(out_kernel, first=first, width=width),
                out_shape=jax.ShapeDtypeStruct((verts, feat), BF16),
                in_specs=[VMEM] * 3,
                out_specs=ANY,
                scratch_shapes=[pltpu.VMEM((verts, feat), BF16), pltpu.SemaphoreType.DMA((verts // width,))],
                name="out",
                **shared,
            )(place, m, fine)
        first += nodes


def spread(x, dom_bits, grps, flip):
    parts = [x]
    bits = dom_bits[:0:-1] + dom_bits[:1]
    for step, bit in enumerate(bits):
        parts.append(flip(x, bit * grps))
        if step + 1 < len(bits):
            x = join(x, parts[-1])
    return x, parts


def layer(
    features,
    w_fine,
    adj_tiles,
    tile_cols,
    tile_count,
    send_lower,
    send_upper,
    assign,
    w_coarse,
    coarse_adj,
):
    verts, _ = features.shape
    block = adj_tiles.shape[2]
    own, nodes = coarse_adj.shape
    doms, grps = lax.axis_size("dom"), lax.axis_size("grp")
    devices = doms * grps
    dom_bits, grp_bits = bits_of(doms), bits_of(grps)
    rows = nodes // doms

    def flip(x, bit):
        return lax.ppermute(x, AXES, [(i, i ^ bit) for i in range(devices)])

    base = 256 // devices + 1
    digits = 1
    while base**digits <= verts:
        digits += 1

    slots = [0]
    for bit in dom_bits[::-1]:
        slots = slots + [s ^ bit for s in slots]

    gather_bits = grp_bits[:1:-1] + grp_bits[:1] + grp_bits[1:2]
    order = [0]
    for bit in gather_bits:
        order = order + [t ^ bit for t in order]
    pieces, coming = [coarse_adj], coarse_adj
    for step, bit in enumerate(gather_bits):
        pieces.append(flip(coming, bit))
        if step + 1 < len(gather_bits):
            coming = join(coming, pieces[-1])

    keep, send, held = segment_sums(features, assign, slots, rows, base, digits)
    for step, bit in enumerate(dom_bits):
        recv = flip(send, bit * grps)
        if step + 1 < len(dom_bits):
            total = keep + recv.astype(F32)
            half = total.shape[0] // 2
            keep, send = total[:half], total[half:].astype(BF16)

    projected, low, up = projection(send_lower, send_upper, held, w_fine, block)
    going_up = [(i, (i + 1) % doms) for i in range(doms)]
    from_below = lax.ppermute(up, "dom", going_up)
    from_above = lax.ppermute(low, "dom", [(j, i) for i, j in going_up])
    fine = fine_rows(tile_cols, tile_count, projected, from_below, from_above, adj_tiles)

    for bit in grp_bits:
        keep = keep + recv.astype(F32)
        recv = flip(keep.astype(BF16), bit)
    proj = coarse_part(keep, recv, w_coarse, rows, base, digits)
    proj, parts = spread(proj, dom_bits, grps, flip)
    mixed = mixed_rows(proj, parts[-1], pieces, slots, rows, own, order)
    _, parts = spread(mixed, dom_bits, grps, flip)
    all_bits = gather_bits + [b * grps for b in dom_bits[:0:-1] + dom_bits[:1]]
    return output_rows(assign, lambda i: parts[i], len(parts), fine, own, all_bits)


def solution(mesh):
    return jax.shard_map(
        layer,
        mesh=mesh,
        in_specs=(
            P(AXES, None),
            P(),
            P(AXES, None, None, None),
            P(AXES, None),
            P(AXES),
            P(AXES),
            P(AXES),
            P(AXES),
            P(),
            P(AXES, None),
        ),
        out_specs=P(AXES, None),
        check_vma=False,
    )
```

profile of v0, /device:TPU:0, one launch (start us, length us, event | category | flops | bytes accessed | tf_op | source)
XLA Modules:
  0.0 64.3 jit_solution(5679365182184675857)
XLA Ops:
  0.0 4.2 %sums.1 = (f32[544,256]{1,0:T(8,128)S(1)}, bf16[544,256]{1,0:T(8,128)(2,1)S(1)}, bf16[4096,256]{1,0:T(8,128)(2,1)S(1)}) custom-call(s32[1,4096]{1,0:T(1,128)} %bitcast.3, bf16[4096,256]{1,0:T(8,128)(2,1)} %x_hbm.1), custom_call_target="tpu_custom_call" | custom-call | flops 2147483648 | bytes 2097152 | tf_op jit(solution)/shard_map/sums/pallas_call | solution.py:105
  4.2 0.0 copy-start.1
  4.2 0.0 copy-start.6
  4.3 0.0 copy-start.7
  4.3 0.6 collective-permute-start
  4.8 1.2 %collective-permute-done = bf16[544,256]{1,0:T(8,128)(2,1)S(1)} collective-permute-done((bf16[544,256]{1,0:T(8,128)(2,1)S(1)}, bf16[544,256]{1,0:T(8,128)(2,1)S(1)}, u32[]{:S(2)}, u32[]{:S(2)}) %collective-permute-start) | collective-permute-done | bytes 278560 | tf_op jit(solution)/shard_map/ppermute | solution.py:485
  6.0 0.1 convert_add_fusion
  6.1 0.0 copy-start.4
  6.1 0.0 copy-start.5
  6.1 2.9 %collective-permute-start.1 = (bf16[272,256]{1,0:T(8,128)(2,1)S(1)}, bf16[272,256]{1,0:T(8,128)(2,1)S(1)}, u32[]{:S(2)}, u32[]{:S(2)}) collective-permute-start(bf16[272,256]{1,0:T(8,128)(2,1)S(1)} %slice.19), channel_id=1, source_target_pairs={{0,16},{1,17},{2,18},{3,19},{4,20},{5,21},{6,22},{7,23},{8,24},{9,... | collective-permute-start | bytes 417800 | tf_op jit(solution)/shard_map/ppermute | solution.py:485
  9.0 4.0 %collective-permute-done.1 = bf16[272,256]{1,0:T(8,128)(2,1)S(1)} collective-permute-done((bf16[272,256]{1,0:T(8,128)(2,1)S(1)}, bf16[272,256]{1,0:T(8,128)(2,1)S(1)}, u32[]{:S(2)}, u32[]{:S(2)}) %collective-permute-start.1) | collective-permute-done | bytes 139296 | tf_op jit(solution)/shard_map/ppermute | solution.py:485
  13.0 1.8 %collective-permute-start.2 = (bf16[272,256]{1,0:T(8,128)(2,1)S(1)}, bf16[272,256]{1,0:T(8,128)(2,1)S(1)}, u32[]{:S(2)}, u32[]{:S(2)}) collective-permute-start(bf16[272,256]{1,0:T(8,128)(2,1)S(1)} %fusion.1), channel_id=1, source_target_pairs={{0,1},{1,0},{2,3},{3,2},{4,5},{5,4},{6,7},{7,6},{8,9},{9,8},{10,11... | collective-permute-start | bytes 417800 | tf_op jit(solution)/shard_map/ppermute | solution.py:485
  14.9 3.4 %collective-permute-done.2 = bf16[272,256]{1,0:T(8,128)(2,1)S(1)} collective-permute-done((bf16[272,256]{1,0:T(8,128)(2,1)S(1)}, bf16[272,256]{1,0:T(8,128)(2,1)S(1)}, u32[]{:S(2)}, u32[]{:S(2)}) %collective-permute-start.2) | collective-permute-done | bytes 139296 | tf_op jit(solution)/shard_map/ppermute | solution.py:485
  18.2 0.1 fusion
  18.3 1.8 %collective-permute-start.3 = (bf16[272,256]{1,0:T(8,128)(2,1)S(1)}, bf16[272,256]{1,0:T(8,128)(2,1)S(1)}, u32[]{:S(2)}, u32[]{:S(2)}) collective-permute-start(bf16[272,256]{1,0:T(8,128)(2,1)S(1)} %fusion), channel_id=1, source_target_pairs={{0,2},{1,3},{2,0},{3,1},{4,6},{5,7},{6,4},{7,5},{8,10},{9,11},{10,... | collective-permute-start | bytes 417800 | tf_op jit(solution)/shard_map/ppermute | solution.py:485
  20.1 3.3 %collective-permute-done.3 = bf16[272,256]{1,0:T(8,128)(2,1)S(1)} collective-permute-done((bf16[272,256]{1,0:T(8,128)(2,1)S(1)}, bf16[272,256]{1,0:T(8,128)(2,1)S(1)}, u32[]{:S(2)}, u32[]{:S(2)}) %collective-permute-start.3) | collective-permute-done | bytes 139296 | tf_op jit(solution)/shard_map/ppermute | solution.py:485
  23.4 0.1 fusion.2
  23.5 3.2 %collective-permute-start.4 = (bf16[272,256]{1,0:T(8,128)(2,1)S(1)}, bf16[272,256]{1,0:T(8,128)(2,1)S(1)}, u32[]{:S(2)}, u32[]{:S(2)}) collective-permute-start(bf16[272,256]{1,0:T(8,128)(2,1)S(1)} %get-tuple-element.21), channel_id=1, source_target_pairs={{0,4},{1,5},{2,6},{3,7},{4,0},{5,1},{6,2},{7,3},{8,12},{9,13},{10,... | collective-permute-start | bytes 417800 | tf_op jit(solution)/shard_map/ppermute | solution.py:485
  26.7 0.0 copy-done
  26.7 0.1 collective-permute-start.7
  26.8 6.6 %collective-permute-done.7.b_ref.refs_3_ = bf16[32,1024]{1,0:T(8,128)(2,1)S(1)} collective-permute-done((bf16[32,1024]{1,0:T(8,128)(2,1)S(1)}, bf16[32,1024]{1,0:T(8,128)(2,1)S(1)}, u32[]{:S(2)}, u32[]{:S(2)}) %collective-permute-start.7) | collective-permute-done | bytes 65568 | tf_op jit(solution)/shard_map/ppermute | solution.py:485
  33.4 1.2 %collective-permute-start.8 = (bf16[64,1024]{1,0:T(8,128)(2,1)S(1)}, bf16[64,1024]{1,0:T(8,128)(2,1)S(1)}, u32[]{:S(2)}, u32[]{:S(2)}) collective-permute-start(bf16[64,1024]{1,0:T(8,128)(2,1)S(1)} %join.5.a_ref), channel_id=1, source_target_pairs={{0,1},{1,0},{2,3},{3,2},{4,5},{5,4},{6,7},{7,6},{8,9},{9,8},{10,11... | collective-permute-start | bytes 393224 | tf_op jit(solution)/shard_map/ppermute | solution.py:485
  34.6 0.0 collective-permute-done.4.recv_ref
  34.6 0.0 copy-done.2
  34.6 0.3 coarse.1.a_ref
  34.9 1.6 %collective-permute-start.5 = (bf16[256,256]{1,0:T(8,128)(2,1)S(1)}, bf16[256,256]{1,0:T(8,128)(2,1)S(1)}, u32[]{:S(2)}, u32[]{:S(2)}) collective-permute-start(bf16[256,256]{1,0:T(8,128)(2,1)S(1)} %coarse.1.a_ref), channel_id=1, source_target_pairs={{0,16},{1,17},{2,18},{3,19},{4,20},{5,21},{6,22},{7,23},{8,24},{9,... | collective-permute-start | bytes 393224 | tf_op jit(solution)/shard_map/ppermute | solution.py:485
  36.4 2.0 %collective-permute-done.8.b_ref.refs_4_ = bf16[64,1024]{1,0:T(8,128)(2,1)S(1)} collective-permute-done((bf16[64,1024]{1,0:T(8,128)(2,1)S(1)}, bf16[64,1024]{1,0:T(8,128)(2,1)S(1)}, u32[]{:S(2)}, u32[]{:S(2)}) %collective-permute-start.8) | collective-permute-done | bytes 131104 | tf_op jit(solution)/shard_map/ppermute | solution.py:485
  38.5 0.3 collective-permute-start.9
  38.8 1.1 %collective-permute-done.5.b_ref = bf16[256,256]{1,0:T(8,128)(2,1)S(1)} collective-permute-done((bf16[256,256]{1,0:T(8,128)(2,1)S(1)}, bf16[256,256]{1,0:T(8,128)(2,1)S(1)}, u32[]{:S(2)}, u32[]{:S(2)}) %collective-permute-start.5) | collective-permute-done | bytes 131104 | tf_op jit(solution)/shard_map/ppermute | solution.py:485
  39.9 0.1 collective-permute-start.6
  40.0 1.3 %proj.1 = (bf16[32,128,256]{2,1,0:T(8,128)(2,1)S(1)}, bf16[4,128,256]{2,1,0:T(8,128)(2,1)S(1)}, bf16[4,128,256]{2,1,0:T(8,128)(2,1)S(1)}) custom-call(s32[4]{0:T(128)S(1)} %copy-done.6, s32[4]{0:T(128)S(1)} %copy-done.7, bf16[4096,256]{1,0:T(8,128)(2,1)S(1)} %get-tuple-element.15.x_ref, bf16[256,256]{1,0:T(8,128)(2,1)S(1)} %copy-done.1), custom_call_target="tpu_custom_call" | custom-call | flops 536870912 | bytes 4194304 | tf_op jit(solution)/shard_map/proj/pallas_call | solution.py:233
  41.3 0.5 collective-permute-start.10
  41.8 1.3 %collective-permute-start.11 = (bf16[4,128,256]{2,1,0:T(8,128)(2,1)S(1)}, bf16[4,128,256]{2,1,0:T(8,128)(2,1)S(1)}, u32[]{:S(2)}, u32[]{:S(2)}) collective-permute-start(bf16[4,128,256]{2,1,0:T(8,128)(2,1)S(1)} %get-tuple-element.18), channel_id=1, source_target_pairs={{8,0},{16,8},{24,16},{0,24},{9,1},{17,9},{25,17},{1,25},{10,2},{18... | collective-permute-start | bytes 786440 | tf_op jit(solution)/shard_map/ppermute | solution.py:517
  43.1 1.8 %collective-permute-done.9.refs_5_ = bf16[128,1024]{1,0:T(8,128)(2,1)S(1)} collective-permute-done((bf16[128,1024]{1,0:T(8,128)(2,1)S(1)}, bf16[128,1024]{1,0:T(8,128)(2,1)S(1)}, u32[]{:S(2)}, u32[]{:S(2)}) %collective-permute-start.9) | collective-permute-done | bytes 262176 | tf_op jit(solution)/shard_map/ppermute | solution.py:485
  44.9 0.0 collective-permute-done.6.refs_1_
  44.9 0.4 mix.1.m_ref.a_ref
  45.3 1.1 %collective-permute-start.12 = (bf16[256,256]{1,0:T(8,128)(2,1)S(1)}, bf16[256,256]{1,0:T(8,128)(2,1)S(1)}, u32[]{:S(2)}, u32[]{:S(2)}) collective-permute-start(bf16[256,256]{1,0:T(8,128)(2,1)S(1)} %mix.1.m_ref.a_ref), channel_id=1, source_target_pairs={{0,16},{1,17},{2,18},{3,19},{4,20},{5,21},{6,22},{7,23},{8,24},{9,... | collective-permute-start | bytes 393224 | tf_op jit(solution)/shard_map/ppermute | solution.py:485
  46.4 6.3 %collective-permute-done.12.b_ref.m_ref = bf16[256,256]{1,0:T(8,128)(2,1)S(1)} collective-permute-done((bf16[256,256]{1,0:T(8,128)(2,1)S(1)}, bf16[256,256]{1,0:T(8,128)(2,1)S(1)}, u32[]{:S(2)}, u32[]{:S(2)}) %collective-permute-start.12) | collective-permute-done | bytes 131104 | tf_op jit(solution)/shard_map/ppermute | solution.py:485
  52.8 0.1 collective-permute-start.13
  52.9 0.0 collective-permute-done.10.below_ref
  52.9 0.0 collective-permute-done.11.above_ref
  52.9 0.0 copy-start.3
  52.9 7.6 %fine.1.fine_ref = f32[4096,256]{1,0:T(8,128)S(1)} custom-call(s32[20,32]{1,0:T(8,128)S(1)} %bitcast.5, s32[32]{0:T(128)S(1)} %copy-done.5, bf16[32,128,256]{2,1,0:T(8,128)(2,1)S(1)} %get-tuple-element.16.own_ref, bf16[4,128,256]{2,1,0:T(8,128)(2,1)S(1)} %collective-permute-done.10.below_ref, bf16[4,128,256]{2,1,0:T(8,128)(2,1)S(1)} %collective-permute-done.11.above_ref, ...), custom_call_target="tpu_custom_call" | custom-call | flops 5368709120 | bytes 20971520 | tf_op jit(solution)/shard_map/fine/pallas_call | solution.py:341
  60.5 0.0 copy-done.3
  60.5 0.8 %place.1 = (f32[4096,256]{1,0:T(8,128)S(1)}, s16[4096,128]{1,0:T(8,128)(2,1)S(1)}) custom-call(s32[32,128]{1,0:T(8,128)S(1)} %bitcast.4, bf16[256,256]{1,0:T(8,128)(2,1)S(1)} %mix.1.m_ref.a_ref, f32[4096,256]{1,0:T(8,128)S(1)} %fine.1.fine_ref), custom_call_target="tpu_custom_call" | custom-call | flops 536870912 | bytes 6291456 | tf_op jit(solution)/shard_map/place/pallas_call | solution.py:424
  61.3 0.7 %gain.1.fine_ref = f32[4096,256]{1,0:T(8,128)S(1)} custom-call(s16[4096,128]{1,0:T(8,128)(2,1)S(1)} %get-tuple-element.19.place_ref, bf16[256,256]{1,0:T(8,128)(2,1)S(1)} %collective-permute-done.12.b_ref.m_ref, f32[4096,256]{1,0:T(8,128)S(1)} %get-tuple-element.20.fine_ref), custom_call_target="tpu_custom_call" | custom-call | flops 536870912 | bytes 6291456 | tf_op jit(solution)/shard_map/gain/pallas_call | solution.py:433
  62.0 0.0 collective-permute-done.13.m_ref
  62.0 2.3 %out.1 = bf16[4096,256]{1,0:T(8,128)(2,1)} custom-call(s16[4096,128]{1,0:T(8,128)(2,1)S(1)} %get-tuple-element.19.place_ref, bf16[512,256]{1,0:T(8,128)(2,1)S(1)} %collective-permute-done.13.m_ref, f32[4096,256]{1,0:T(8,128)S(1)} %gain.1.fine_ref), custom_call_target="tpu_custom_call" | custom-call | flops 1073741824 | bytes 6291456 | tf_op jit(solution)/shard_map/out/pallas_call | solution.py:442
  (13 shorter events, 0.1 us)
Async XLA Ops:
  0.0 26.7 %copy-start = (bf16[32,1024]{1,0:T(8,128)(2,1)S(1)}, bf16[32,1024]{1,0:T(8,128)(2,1)}, u32[]{:S(2)}) copy-start(bf16[32,1024]{1,0:T(8,128)(2,1)} %refs_2_.1) | copy-start | bytes 196612
  0.0 34.6 %copy-start.2 = (bf16[256,256]{1,0:T(8,128)(2,1)S(1)}, bf16[256,256]{1,0:T(8,128)(2,1)}, u32[]{:S(2)}) copy-start(bf16[256,256]{1,0:T(8,128)(2,1)} %w_ref.2) | copy-start | bytes 393220
  4.2 35.8 %copy-start.1 = (bf16[256,256]{1,0:T(8,128)(2,1)S(1)}, bf16[256,256]{1,0:T(8,128)(2,1)}, u32[]{:S(2)}) copy-start(bf16[256,256]{1,0:T(8,128)(2,1)} %w_ref.3) | copy-start | bytes 393220
  4.2 35.8 %copy-start.6 = (s32[4]{0:T(128)S(1)}, s32[4]{0:T(128)}, u32[]{:S(2)}) copy-start(s32[4]{0:T(128)} %low_idx.1) | copy-start | bytes 52
  4.3 35.8 %copy-start.7 = (s32[4]{0:T(128)S(1)}, s32[4]{0:T(128)}, u32[]{:S(2)}) copy-start(s32[4]{0:T(128)} %up_idx.1) | copy-start | bytes 52
  4.3 1.7 %collective-permute-start = (bf16[544,256]{1,0:T(8,128)(2,1)S(1)}, bf16[544,256]{1,0:T(8,128)(2,1)S(1)}, u32[]{:S(2)}, u32[]{:S(2)}) collective-permute-start(bf16[544,256]{1,0:T(8,128)(2,1)S(1)} %get-tuple-element.14), channel_id=1, source_target_pairs={{0,8},{1,9},{2,10},{3,11},{4,12},{5,13},{6,14},{7,15},{8,0},{9,1},... | collective-permute-start | bytes 835592 | tf_op jit(solution)/shard_map/ppermute | solution.py:485
  6.1 46.8 %copy-start.4 = (s32[32,20]{0,1:T(8,128)S(1)}, s32[32,20]{0,1:T(8,128)}, u32[]{:S(2)}) copy-start(s32[32,20]{0,1:T(8,128)} %param.13) | copy-start | bytes 7684
  6.1 46.8 %copy-start.5 = (s32[32]{0:T(128)S(1)}, s32[32]{0:T(128)}, u32[]{:S(2)}) copy-start(s32[32]{0:T(128)} %live_ref.1) | copy-start | bytes 388
  6.1 6.9 %collective-permute-start.1 = (bf16[272,256]{1,0:T(8,128)(2,1)S(1)}, bf16[272,256]{1,0:T(8,128)(2,1)S(1)}, u32[]{:S(2)}, u32[]{:S(2)}) collective-permute-start(bf16[272,256]{1,0:T(8,128)(2,1)S(1)} %slice.19), channel_id=1, source_target_pairs={{0,16},{1,17},{2,18},{3,19},{4,20},{5,21},{6,22},{7,23},{8,24},{9,... | collective-permute-start | bytes 417800 | tf_op jit(solution)/shard_map/ppermute | solution.py:485
  13.0 5.2 %collective-permute-start.2 = (bf16[272,256]{1,0:T(8,128)(2,1)S(1)}, bf16[272,256]{1,0:T(8,128)(2,1)S(1)}, u32[]{:S(2)}, u32[]{:S(2)}) collective-permute-start(bf16[272,256]{1,0:T(8,128)(2,1)S(1)} %fusion.1), channel_id=1, source_target_pairs={{0,1},{1,0},{2,3},{3,2},{4,5},{5,4},{6,7},{7,6},{8,9},{9,8},{10,11... | collective-permute-start | bytes 417800 | tf_op jit(solution)/shard_map/ppermute | solution.py:485
  18.3 5.1 %collective-permute-start.3 = (bf16[272,256]{1,0:T(8,128)(2,1)S(1)}, bf16[272,256]{1,0:T(8,128)(2,1)S(1)}, u32[]{:S(2)}, u32[]{:S(2)}) collective-permute-start(bf16[272,256]{1,0:T(8,128)(2,1)S(1)} %fusion), channel_id=1, source_target_pairs={{0,2},{1,3},{2,0},{3,1},{4,6},{5,7},{6,4},{7,5},{8,10},{9,11},{10,... | collective-permute-start | bytes 417800 | tf_op jit(solution)/shard_map/ppermute | solution.py:485
  23.5 11.1 %collective-permute-start.4 = (bf16[272,256]{1,0:T(8,128)(2,1)S(1)}, bf16[272,256]{1,0:T(8,128)(2,1)S(1)}, u32[]{:S(2)}, u32[]{:S(2)}) collective-permute-start(bf16[272,256]{1,0:T(8,128)(2,1)S(1)} %get-tuple-element.21), channel_id=1, source_target_pairs={{0,4},{1,5},{2,6},{3,7},{4,0},{5,1},{6,2},{7,3},{8,12},{9,13},{10,... | collective-permute-start | bytes 417800 | tf_op jit(solution)/shard_map/ppermute | solution.py:485
  26.7 6.7 %collective-permute-start.7 = (bf16[32,1024]{1,0:T(8,128)(2,1)S(1)}, bf16[32,1024]{1,0:T(8,128)(2,1)S(1)}, u32[]{:S(2)}, u32[]{:S(2)}) collective-permute-start(bf16[32,1024]{1,0:T(8,128)(2,1)S(1)} %copy-done), channel_id=1, source_target_pairs={{0,4},{1,5},{2,6},{3,7},{4,0},{5,1},{6,2},{7,3},{8,12},{9,13},{10,... | collective-permute-start | bytes 196616 | tf_op jit(solution)/shard_map/ppermute | solution.py:485
  33.4 5.0 %collective-permute-start.8 = (bf16[64,1024]{1,0:T(8,128)(2,1)S(1)}, bf16[64,1024]{1,0:T(8,128)(2,1)S(1)}, u32[]{:S(2)}, u32[]{:S(2)}) collective-permute-start(bf16[64,1024]{1,0:T(8,128)(2,1)S(1)} %join.5.a_ref), channel_id=1, source_target_pairs={{0,1},{1,0},{2,3},{3,2},{4,5},{5,4},{6,7},{7,6},{8,9},{9,8},{10,11... | collective-permute-start | bytes 393224 | tf_op jit(solution)/shard_map/ppermute | solution.py:485
  34.9 5.0 %collective-permute-start.5 = (bf16[256,256]{1,0:T(8,128)(2,1)S(1)}, bf16[256,256]{1,0:T(8,128)(2,1)S(1)}, u32[]{:S(2)}, u32[]{:S(2)}) collective-permute-start(bf16[256,256]{1,0:T(8,128)(2,1)S(1)} %coarse.1.a_ref), channel_id=1, source_target_pairs={{0,16},{1,17},{2,18},{3,19},{4,20},{5,21},{6,22},{7,23},{8,24},{9,... | collective-permute-start | bytes 393224 | tf_op jit(solution)/shard_map/ppermute | solution.py:485
  38.5 6.4 %collective-permute-start.9 = (bf16[128,1024]{1,0:T(8,128)(2,1)S(1)}, bf16[128,1024]{1,0:T(8,128)(2,1)S(1)}, u32[]{:S(2)}, u32[]{:S(2)}) collective-permute-start(bf16[128,1024]{1,0:T(8,128)(2,1)S(1)} %join.6), channel_id=1, source_target_pairs={{0,2},{1,3},{2,0},{3,1},{4,6},{5,7},{6,4},{7,5},{8,10},{9,11},{10,... | collective-permute-start | bytes 786440 | tf_op jit(solution)/shard_map/ppermute | solution.py:485
  39.9 5.0 %collective-permute-start.6 = (bf16[512,256]{1,0:T(8,128)(2,1)S(1)}, bf16[512,256]{1,0:T(8,128)(2,1)S(1)}, u32[]{:S(2)}, u32[]{:S(2)}) collective-permute-start(bf16[512,256]{1,0:T(8,128)(2,1)S(1)} %join.4.refs_0_), channel_id=1, source_target_pairs={{0,8},{1,9},{2,10},{3,11},{4,12},{5,13},{6,14},{7,15},{8,0},{9,1},... | collective-permute-start | bytes 786440 | tf_op jit(solution)/shard_map/ppermute | solution.py:485
  41.3 11.6 %collective-permute-start.10 = (bf16[4,128,256]{2,1,0:T(8,128)(2,1)S(1)}, bf16[4,128,256]{2,1,0:T(8,128)(2,1)S(1)}, u32[]{:S(2)}, u32[]{:S(2)}) collective-permute-start(bf16[4,128,256]{2,1,0:T(8,128)(2,1)S(1)} %get-tuple-element.17), channel_id=1, source_target_pairs={{0,8},{8,16},{16,24},{24,0},{1,9},{9,17},{17,25},{25,1},{2,10},{10... | collective-permute-start | bytes 786440 | tf_op jit(solution)/shard_map/ppermute | solution.py:516
  41.8 11.1 %collective-permute-start.11 = (bf16[4,128,256]{2,1,0:T(8,128)(2,1)S(1)}, bf16[4,128,256]{2,1,0:T(8,128)(2,1)S(1)}, u32[]{:S(2)}, u32[]{:S(2)}) collective-permute-start(bf16[4,128,256]{2,1,0:T(8,128)(2,1)S(1)} %get-tuple-element.18), channel_id=1, source_target_pairs={{8,0},{16,8},{24,16},{0,24},{9,1},{17,9},{25,17},{1,25},{10,2},{18... | collective-permute-start | bytes 786440 | tf_op jit(solution)/shard_map/ppermute | solution.py:517
  45.3 7.5 %collective-permute-start.12 = (bf16[256,256]{1,0:T(8,128)(2,1)S(1)}, bf16[256,256]{1,0:T(8,128)(2,1)S(1)}, u32[]{:S(2)}, u32[]{:S(2)}) collective-permute-start(bf16[256,256]{1,0:T(8,128)(2,1)S(1)} %mix.1.m_ref.a_ref), channel_id=1, source_target_pairs={{0,16},{1,17},{2,18},{3,19},{4,20},{5,21},{6,22},{7,23},{8,24},{9,... | collective-permute-start | bytes 393224 | tf_op jit(solution)/shard_map/ppermute | solution.py:485
  52.8 9.2 %collective-permute-start.13 = (bf16[512,256]{1,0:T(8,128)(2,1)S(1)}, bf16[512,256]{1,0:T(8,128)(2,1)S(1)}, u32[]{:S(2)}, u32[]{:S(2)}) collective-permute-start(bf16[512,256]{1,0:T(8,128)(2,1)S(1)} %join.7), channel_id=1, source_target_pairs={{0,8},{1,9},{2,10},{3,11},{4,12},{5,13},{6,14},{7,15},{8,0},{9,1},... | collective-permute-start | bytes 786440 | tf_op jit(solution)/shard_map/ppermute | solution.py:485
  52.9 7.6 %copy-start.3 = (s32[4096]{0:T(1024)S(1)}, s32[4096]{0:T(1024)}, u32[]{:S(2)}) copy-start(s32[4096]{0:T(1024)} %param.17) | copy-start | bytes 49156
where the time goes:
time: 65.4 us; the launch traced here: 64.3 us
  waiting for transfers between devices  29.7 us (45%)
  Pallas kernels  17.6 us (27%)
  starting transfers between devices  16.6 us (25%)
    ppermute x12, waiting for transfers between devices, flip(): return lax.ppermute(x, AXES, [(i, i ^ bit) for i in range(devices)])  29.7 us
    ppermute x12, starting transfers between devices, flip(): return lax.ppermute(x, AXES, [(i, i ^ bit) for i in range(devices)])  14.8 us
    pallas_call x1, Pallas kernels, fine_rows(): pl.pallas_call(fine_kernel, out_shape=jax.ShapeDtypeStruct((rows * block,...  7.58 us
    pallas_call x1, Pallas kernels, segment_sums(): pl.pallas_call(functools.partial(sums_kernel, slots=slots, rows=rows, bas...  4.21 us
    pallas_call x1, Pallas kernels, output_rows(): pl.pallas_call(functools.partial(out_kernel, first=first, width=width), o...  2.28 us
  transfers between devices with their start and end apart: 14, of which 9 were waited for; matrix products, arithmetic and copies ran while one was open for 0% of the time, Pallas kernels for 17%

commit v1 on v0

--- a/solution.py
+++ b/solution.py
@@ -98,7 +98,7 @@
 
 def segment_sums(features, assign, slots, rows, base, digits):
     verts, feat = features.shape
-    width = min(verts, 1024)
+    width = min(verts, 2048)
     half = len(slots) // 2
     shape = (half * (rows + EXTRA), feat)
     nodes = len(slots) * rows
@@ -253,15 +253,15 @@
     def groups(r):
         return lax.div(live_ref[r] + (GROUP - 1), GROUP)
 
-    def fetch(r, i):
-        at = pl.ds(i * GROUP, GROUP)
-        return pltpu.make_async_copy(adj_hbm.at[r, at], tiles.at[r, at], sems.at[r, i])
+    most = tiles.shape[1] // GROUP
+
+    def fetch(r, count):
+        at = pl.ds(0, count * GROUP)
+        return pltpu.make_async_copy(adj_hbm.at[r, at], tiles.at[r, at], sems.at[r])
 
     @pl.loop(0, rows)
     def _(r):
-        @pl.loop(0, groups(r))
-        def _(i):
-            fetch(r, i).start()
+        lax.switch(groups(r) - 1, [lambda n=n: fetch(r, n).start() for n in range(1, most + 1)])
 
     ext[0:rows] = own_ref[...]
     ext[rows : rows + halo] = below_ref[...]
@@ -286,8 +286,7 @@
 
             def with_groups(count):
                 def run():
-                    for i in range(count):
-                        fetch(r, i).wait()
+                    fetch(r, count).wait()
                     for i in range(count):
                         coming = columns_of(following, 0) if i + 1 == count else columns_of(r, i + 1)
                         for q in range(2):
@@ -306,7 +305,7 @@
 
                 return run
 
-            lax.switch(groups(r) - 1, [with_groups(n + 1) for n in range(cols_ref.shape[0] // GROUP)])
+            lax.switch(groups(r) - 1, [with_groups(n) for n in range(1, most + 1)])
 
         push(columns_of(0, 0))
         for r in range(LAG):
@@ -346,7 +345,7 @@
         scratch_shapes=[
             pltpu.VMEM((rows + 2 * halo, block, feat), BF16),
             pltpu.VMEM((rows, slots, block, block), BF16),
-            pltpu.SemaphoreType.DMA((rows, slots // GROUP)),
+            pltpu.SemaphoreType.DMA((rows,)),
         ],
         compiler_params=pltpu.CompilerParams(vmem_limit_bytes=36 << 20),
         cost_estimate=cost(2 * rows * slots * block * block * feat, rows * slots * block * block * 2),

time: 65.4 us -> 63.5 us (0.971)
  Pallas kernels: 17.6 us -> 16 us
    pallas_call x1, Pallas kernels: 7.58 us -> 6.2 us  [fine_rows(): pl.pallas_call(fine_kernel, out_shape=jax.ShapeDtypeStruct((rows * block,...]
  transfers between devices with their start and end apart: 14 -> 14, of which waited for: 9 -> 9; matrix products, arithmetic and copies ran while one was open for 0% -> 0% of each run, Pallas kernels for 17% -> 15%
where the time goes in v1:
time: 63.5 us; the launch traced here: 62.7 us
  waiting for transfers between devices  29.7 us (47%)
  starting transfers between devices  16.6 us (26%)
  Pallas kernels  16 us (25%)
    ppermute x12, waiting for transfers between devices, flip(): return lax.ppermute(x, AXES, [(i, i ^ bit) for i in range(devices)])  29.7 us
    ppermute x12, starting transfers between devices, flip(): return lax.ppermute(x, AXES, [(i, i ^ bit) for i in range(devices)])  14.8 us
    pallas_call x1, Pallas kernels, fine_rows(): pl.pallas_call(fine_kernel, out_shape=jax.ShapeDtypeStruct((rows * block,...  6.2 us
    pallas_call x1, Pallas kernels, segment_sums(): pl.pallas_call(functools.partial(sums_kernel, slots=slots, rows=rows, bas...  3.98 us
    pallas_call x1, Pallas kernels, output_rows(): pl.pallas_call(functools.partial(out_kernel, first=first, width=width), o...  2.28 us
    pallas_call x1, Pallas kernels, projection(): pl.pallas_call(functools.partial(proj_kernel, width=min(verts, 1024)), ou...  1.29 us
    ppermute x1, starting transfers between devices, layer(): from_above = lax.ppermute(low, 'dom', [(j, i) for i, j in going_up])  1.27 us
  transfers between devices with their start and end apart: 14, of which 9 were waited for; matrix products, arithmetic and copies ran while one was open for 0% of the time, Pallas kernels for 15%

profile of v1, /device:TPU:0, one launch (start us, length us, event | category | flops | bytes accessed | tf_op | source)
XLA Modules:
  0.0 62.7 jit_solution(11994406945851668023)
XLA Ops:
  0.0 4.0 %sums.1 = (f32[544,256]{1,0:T(8,128)S(1)}, bf16[544,256]{1,0:T(8,128)(2,1)S(1)}, bf16[4096,256]{1,0:T(8,128)(2,1)S(1)}) custom-call(s32[1,4096]{1,0:T(1,128)} %bitcast.3, bf16[4096,256]{1,0:T(8,128)(2,1)} %x_hbm.1), custom_call_target="tpu_custom_call" | custom-call | flops 2147483648 | bytes 2097152 | tf_op jit(solution)/shard_map/sums/pallas_call | solution.py:105
  4.0 0.0 copy-start.1
  4.0 0.0 copy-start.6
  4.0 0.0 copy-start.7
  4.0 0.6 collective-permute-start
  4.6 1.2 %collective-permute-done = bf16[544,256]{1,0:T(8,128)(2,1)S(1)} collective-permute-done((bf16[544,256]{1,0:T(8,128)(2,1)S(1)}, bf16[544,256]{1,0:T(8,128)(2,1)S(1)}, u32[]{:S(2)}, u32[]{:S(2)}) %collective-permute-start) | collective-permute-done | bytes 278560 | tf_op jit(solution)/shard_map/ppermute | solution.py:484
  5.8 0.1 convert_add_fusion
  5.9 0.0 copy-start.4
  5.9 0.0 copy-start.5
  5.9 2.9 %collective-permute-start.1 = (bf16[272,256]{1,0:T(8,128)(2,1)S(1)}, bf16[272,256]{1,0:T(8,128)(2,1)S(1)}, u32[]{:S(2)}, u32[]{:S(2)}) collective-permute-start(bf16[272,256]{1,0:T(8,128)(2,1)S(1)} %slice.19), channel_id=1, source_target_pairs={{0,16},{1,17},{2,18},{3,19},{4,20},{5,21},{6,22},{7,23},{8,24},{9,... | collective-permute-start | bytes 417800 | tf_op jit(solution)/shard_map/ppermute | solution.py:484
  8.8 4.0 %collective-permute-done.1 = bf16[272,256]{1,0:T(8,128)(2,1)S(1)} collective-permute-done((bf16[272,256]{1,0:T(8,128)(2,1)S(1)}, bf16[272,256]{1,0:T(8,128)(2,1)S(1)}, u32[]{:S(2)}, u32[]{:S(2)}) %collective-permute-start.1) | collective-permute-done | bytes 139296 | tf_op jit(solution)/shard_map/ppermute | solution.py:484
  12.8 1.8 %collective-permute-start.2 = (bf16[272,256]{1,0:T(8,128)(2,1)S(1)}, bf16[272,256]{1,0:T(8,128)(2,1)S(1)}, u32[]{:S(2)}, u32[]{:S(2)}) collective-permute-start(bf16[272,256]{1,0:T(8,128)(2,1)S(1)} %fusion.1), channel_id=1, source_target_pairs={{0,1},{1,0},{2,3},{3,2},{4,5},{5,4},{6,7},{7,6},{8,9},{9,8},{10,11... | collective-permute-start | bytes 417800 | tf_op jit(solution)/shard_map/ppermute | solution.py:484
  14.6 3.4 %collective-permute-done.2 = bf16[272,256]{1,0:T(8,128)(2,1)S(1)} collective-permute-done((bf16[272,256]{1,0:T(8,128)(2,1)S(1)}, bf16[272,256]{1,0:T(8,128)(2,1)S(1)}, u32[]{:S(2)}, u32[]{:S(2)}) %collective-permute-start.2) | collective-permute-done | bytes 139296 | tf_op jit(solution)/shard_map/ppermute | solution.py:484
  18.0 0.1 fusion
  18.1 1.8 %collective-permute-start.3 = (bf16[272,256]{1,0:T(8,128)(2,1)S(1)}, bf16[272,256]{1,0:T(8,128)(2,1)S(1)}, u32[]{:S(2)}, u32[]{:S(2)}) collective-permute-start(bf16[272,256]{1,0:T(8,128)(2,1)S(1)} %fusion), channel_id=1, source_target_pairs={{0,2},{1,3},{2,0},{3,1},{4,6},{5,7},{6,4},{7,5},{8,10},{9,11},{10,... | collective-permute-start | bytes 417800 | tf_op jit(solution)/shard_map/ppermute | solution.py:484
  19.9 3.3 %collective-permute-done.3 = bf16[272,256]{1,0:T(8,128)(2,1)S(1)} collective-permute-done((bf16[272,256]{1,0:T(8,128)(2,1)S(1)}, bf16[272,256]{1,0:T(8,128)(2,1)S(1)}, u32[]{:S(2)}, u32[]{:S(2)}) %collective-permute-start.3) | collective-permute-done | bytes 139296 | tf_op jit(solution)/shard_map/ppermute | solution.py:484
  23.2 0.1 fusion.2
  23.3 3.2 %collective-permute-start.4 = (bf16[272,256]{1,0:T(8,128)(2,1)S(1)}, bf16[272,256]{1,0:T(8,128)(2,1)S(1)}, u32[]{:S(2)}, u32[]{:S(2)}) collective-permute-start(bf16[272,256]{1,0:T(8,128)(2,1)S(1)} %get-tuple-element.21), channel_id=1, source_target_pairs={{0,4},{1,5},{2,6},{3,7},{4,0},{5,1},{6,2},{7,3},{8,12},{9,13},{10,... | collective-permute-start | bytes 417800 | tf_op jit(solution)/shard_map/ppermute | solution.py:484
  26.5 0.0 copy-done
  26.5 0.1 collective-permute-start.7
  26.6 6.6 %collective-permute-done.7.b_ref.refs_3_ = bf16[32,1024]{1,0:T(8,128)(2,1)S(1)} collective-permute-done((bf16[32,1024]{1,0:T(8,128)(2,1)S(1)}, bf16[32,1024]{1,0:T(8,128)(2,1)S(1)}, u32[]{:S(2)}, u32[]{:S(2)}) %collective-permute-start.7) | collective-permute-done | bytes 65568 | tf_op jit(solution)/shard_map/ppermute | solution.py:484
  33.2 1.2 %collective-permute-start.8 = (bf16[64,1024]{1,0:T(8,128)(2,1)S(1)}, bf16[64,1024]{1,0:T(8,128)(2,1)S(1)}, u32[]{:S(2)}, u32[]{:S(2)}) collective-permute-start(bf16[64,1024]{1,0:T(8,128)(2,1)S(1)} %join.5.a_ref), channel_id=1, source_target_pairs={{0,1},{1,0},{2,3},{3,2},{4,5},{5,4},{6,7},{7,6},{8,9},{9,8},{10,11... | collective-permute-start | bytes 393224 | tf_op jit(solution)/shard_map/ppermute | solution.py:484
  34.3 0.0 collective-permute-done.4.recv_ref
  34.3 0.0 copy-done.2
  34.3 0.3 coarse.1.a_ref
  34.6 1.6 %collective-permute-start.5 = (bf16[256,256]{1,0:T(8,128)(2,1)S(1)}, bf16[256,256]{1,0:T(8,128)(2,1)S(1)}, u32[]{:S(2)}, u32[]{:S(2)}) collective-permute-start(bf16[256,256]{1,0:T(8,128)(2,1)S(1)} %coarse.1.a_ref), channel_id=1, source_target_pairs={{0,16},{1,17},{2,18},{3,19},{4,20},{5,21},{6,22},{7,23},{8,24},{9,... | collective-permute-start | bytes 393224 | tf_op jit(solution)/shard_map/ppermute | solution.py:484
  36.2 2.0 %collective-permute-done.8.b_ref.refs_4_ = bf16[64,1024]{1,0:T(8,128)(2,1)S(1)} collective-permute-done((bf16[64,1024]{1,0:T(8,128)(2,1)S(1)}, bf16[64,1024]{1,0:T(8,128)(2,1)S(1)}, u32[]{:S(2)}, u32[]{:S(2)}) %collective-permute-start.8) | collective-permute-done | bytes 131104 | tf_op jit(solution)/shard_map/ppermute | solution.py:484
  38.2 0.3 collective-permute-start.9
  38.5 1.1 %collective-permute-done.5.b_ref = bf16[256,256]{1,0:T(8,128)(2,1)S(1)} collective-permute-done((bf16[256,256]{1,0:T(8,128)(2,1)S(1)}, bf16[256,256]{1,0:T(8,128)(2,1)S(1)}, u32[]{:S(2)}, u32[]{:S(2)}) %collective-permute-start.5) | collective-permute-done | bytes 131104 | tf_op jit(solution)/shard_map/ppermute | solution.py:484
  39.7 0.1 collective-permute-start.6
  39.8 1.3 %proj.1 = (bf16[32,128,256]{2,1,0:T(8,128)(2,1)S(1)}, bf16[4,128,256]{2,1,0:T(8,128)(2,1)S(1)}, bf16[4,128,256]{2,1,0:T(8,128)(2,1)S(1)}) custom-call(s32[4]{0:T(128)S(1)} %copy-done.6, s32[4]{0:T(128)S(1)} %copy-done.7, bf16[4096,256]{1,0:T(8,128)(2,1)S(1)} %get-tuple-element.15.x_ref, bf16[256,256]{1,0:T(8,128)(2,1)S(1)} %copy-done.1), custom_call_target="tpu_custom_call" | custom-call | flops 536870912 | bytes 4194304 | tf_op jit(solution)/shard_map/proj/pallas_call | solution.py:233
  41.1 0.5 collective-permute-start.10
  41.6 1.3 %collective-permute-start.11 = (bf16[4,128,256]{2,1,0:T(8,128)(2,1)S(1)}, bf16[4,128,256]{2,1,0:T(8,128)(2,1)S(1)}, u32[]{:S(2)}, u32[]{:S(2)}) collective-permute-start(bf16[4,128,256]{2,1,0:T(8,128)(2,1)S(1)} %get-tuple-element.18), channel_id=1, source_target_pairs={{8,0},{16,8},{24,16},{0,24},{9,1},{17,9},{25,17},{1,25},{10,2},{18... | collective-permute-start | bytes 786440 | tf_op jit(solution)/shard_map/ppermute | solution.py:516
  42.9 1.8 %collective-permute-done.9.refs_5_ = bf16[128,1024]{1,0:T(8,128)(2,1)S(1)} collective-permute-done((bf16[128,1024]{1,0:T(8,128)(2,1)S(1)}, bf16[128,1024]{1,0:T(8,128)(2,1)S(1)}, u32[]{:S(2)}, u32[]{:S(2)}) %collective-permute-start.9) | collective-permute-done | bytes 262176 | tf_op jit(solution)/shard_map/ppermute | solution.py:484
  44.7 0.0 collective-permute-done.6.refs_1_
  44.7 0.4 mix.1.m_ref.a_ref
  45.1 1.1 %collective-permute-start.12 = (bf16[256,256]{1,0:T(8,128)(2,1)S(1)}, bf16[256,256]{1,0:T(8,128)(2,1)S(1)}, u32[]{:S(2)}, u32[]{:S(2)}) collective-permute-start(bf16[256,256]{1,0:T(8,128)(2,1)S(1)} %mix.1.m_ref.a_ref), channel_id=1, source_target_pairs={{0,16},{1,17},{2,18},{3,19},{4,20},{5,21},{6,22},{7,23},{8,24},{9,... | collective-permute-start | bytes 393224 | tf_op jit(solution)/shard_map/ppermute | solution.py:484
  46.2 6.3 %collective-permute-done.12.b_ref.m_ref = bf16[256,256]{1,0:T(8,128)(2,1)S(1)} collective-permute-done((bf16[256,256]{1,0:T(8,128)(2,1)S(1)}, bf16[256,256]{1,0:T(8,128)(2,1)S(1)}, u32[]{:S(2)}, u32[]{:S(2)}) %collective-permute-start.12) | collective-permute-done | bytes 131104 | tf_op jit(solution)/shard_map/ppermute | solution.py:484
  52.6 0.1 collective-permute-start.13
  52.6 0.0 collective-permute-done.10.below_ref
  52.7 0.0 collective-permute-done.11.above_ref
  52.7 0.0 copy-start.3
  52.7 6.2 %fine.1.fine_ref = f32[4096,256]{1,0:T(8,128)S(1)} custom-call(s32[20,32]{1,0:T(8,128)S(1)} %bitcast.5, s32[32]{0:T(128)S(1)} %copy-done.5, bf16[32,128,256]{2,1,0:T(8,128)(2,1)S(1)} %get-tuple-element.16.own_ref, bf16[4,128,256]{2,1,0:T(8,128)(2,1)S(1)} %collective-permute-done.10.below_ref, bf16[4,128,256]{2,1,0:T(8,128)(2,1)S(1)} %collective-permute-done.11.above_ref, ...), custom_call_target="tpu_custom_call" | custom-call | flops 5368709120 | bytes 20971520 | tf_op jit(solution)/shard_map/fine/pallas_call | solution.py:340
  58.9 0.0 copy-done.3
  58.9 0.8 %place.1 = (f32[4096,256]{1,0:T(8,128)S(1)}, s16[4096,128]{1,0:T(8,128)(2,1)S(1)}) custom-call(s32[32,128]{1,0:T(8,128)S(1)} %bitcast.4, bf16[256,256]{1,0:T(8,128)(2,1)S(1)} %mix.1.m_ref.a_ref, f32[4096,256]{1,0:T(8,128)S(1)} %fine.1.fine_ref), custom_call_target="tpu_custom_call" | custom-call | flops 536870912 | bytes 6291456 | tf_op jit(solution)/shard_map/place/pallas_call | solution.py:423
  59.7 0.7 %gain.1.fine_ref = f32[4096,256]{1,0:T(8,128)S(1)} custom-call(s16[4096,128]{1,0:T(8,128)(2,1)S(1)} %get-tuple-element.19.place_ref, bf16[256,256]{1,0:T(8,128)(2,1)S(1)} %collective-permute-done.12.b_ref.m_ref, f32[4096,256]{1,0:T(8,128)S(1)} %get-tuple-element.20.fine_ref), custom_call_target="tpu_custom_call" | custom-call | flops 536870912 | bytes 6291456 | tf_op jit(solution)/shard_map/gain/pallas_call | solution.py:432
  60.4 0.0 collective-permute-done.13.m_ref
  60.4 2.3 %out.1 = bf16[4096,256]{1,0:T(8,128)(2,1)} custom-call(s16[4096,128]{1,0:T(8,128)(2,1)S(1)} %get-tuple-element.19.place_ref, bf16[512,256]{1,0:T(8,128)(2,1)S(1)} %collective-permute-done.13.m_ref, f32[4096,256]{1,0:T(8,128)S(1)} %gain.1.fine_ref), custom_call_target="tpu_custom_call" | custom-call | flops 1073741824 | bytes 6291456 | tf_op jit(solution)/shard_map/out/pallas_call | solution.py:441
  (13 shorter events, 0.1 us)
Async XLA Ops:
  0.0 26.5 %copy-start = (bf16[32,1024]{1,0:T(8,128)(2,1)S(1)}, bf16[32,1024]{1,0:T(8,128)(2,1)}, u32[]{:S(2)}) copy-start(bf16[32,1024]{1,0:T(8,128)(2,1)} %refs_2_.1) | copy-start | bytes 196612
  0.0 34.3 %copy-start.2 = (bf16[256,256]{1,0:T(8,128)(2,1)S(1)}, bf16[256,256]{1,0:T(8,128)(2,1)}, u32[]{:S(2)}) copy-start(bf16[256,256]{1,0:T(8,128)(2,1)} %w_ref.2) | copy-start | bytes 393220
  4.0 35.8 %copy-start.1 = (bf16[256,256]{1,0:T(8,128)(2,1)S(1)}, bf16[256,256]{1,0:T(8,128)(2,1)}, u32[]{:S(2)}) copy-start(bf16[256,256]{1,0:T(8,128)(2,1)} %w_ref.3) | copy-start | bytes 393220
  4.0 35.8 %copy-start.6 = (s32[4]{0:T(128)S(1)}, s32[4]{0:T(128)}, u32[]{:S(2)}) copy-start(s32[4]{0:T(128)} %low_idx.1) | copy-start | bytes 52
  4.0 35.8 %copy-start.7 = (s32[4]{0:T(128)S(1)}, s32[4]{0:T(128)}, u32[]{:S(2)}) copy-start(s32[4]{0:T(128)} %up_idx.1) | copy-start | bytes 52
  4.0 1.7 %collective-permute-start = (bf16[544,256]{1,0:T(8,128)(2,1)S(1)}, bf16[544,256]{1,0:T(8,128)(2,1)S(1)}, u32[]{:S(2)}, u32[]{:S(2)}) collective-permute-start(bf16[544,256]{1,0:T(8,128)(2,1)S(1)} %get-tuple-element.14), channel_id=1, source_target_pairs={{0,8},{1,9},{2,10},{3,11},{4,12},{5,13},{6,14},{7,15},{8,0},{9,1},... | collective-permute-start | bytes 835592 | tf_op jit(solution)/shard_map/ppermute | solution.py:484
  5.9 46.8 %copy-start.4 = (s32[32,20]{0,1:T(8,128)S(1)}, s32[32,20]{0,1:T(8,128)}, u32[]{:S(2)}) copy-start(s32[32,20]{0,1:T(8,128)} %param.13) | copy-start | bytes 7684
  5.9 46.8 %copy-start.5 = (s32[32]{0:T(128)S(1)}, s32[32]{0:T(128)}, u32[]{:S(2)}) copy-start(s32[32]{0:T(128)} %live_ref.1) | copy-start | bytes 388
  5.9 6.9 %collective-permute-start.1 = (bf16[272,256]{1,0:T(8,128)(2,1)S(1)}, bf16[272,256]{1,0:T(8,128)(2,1)S(1)}, u32[]{:S(2)}, u32[]{:S(2)}) collective-permute-start(bf16[272,256]{1,0:T(8,128)(2,1)S(1)} %slice.19), channel_id=1, source_target_pairs={{0,16},{1,17},{2,18},{3,19},{4,20},{5,21},{6,22},{7,23},{8,24},{9,... | collective-permute-start | bytes 417800 | tf_op jit(solution)/shard_map/ppermute | solution.py:484
  12.8 5.2 %collective-permute-start.2 = (bf16[272,256]{1,0:T(8,128)(2,1)S(1)}, bf16[272,256]{1,0:T(8,128)(2,1)S(1)}, u32[]{:S(2)}, u32[]{:S(2)}) collective-permute-start(bf16[272,256]{1,0:T(8,128)(2,1)S(1)} %fusion.1), channel_id=1, source_target_pairs={{0,1},{1,0},{2,3},{3,2},{4,5},{5,4},{6,7},{7,6},{8,9},{9,8},{10,11... | collective-permute-start | bytes 417800 | tf_op jit(solution)/shard_map/ppermute | solution.py:484
  18.1 5.1 %collective-permute-start.3 = (bf16[272,256]{1,0:T(8,128)(2,1)S(1)}, bf16[272,256]{1,0:T(8,128)(2,1)S(1)}, u32[]{:S(2)}, u32[]{:S(2)}) collective-permute-start(bf16[272,256]{1,0:T(8,128)(2,1)S(1)} %fusion), channel_id=1, source_target_pairs={{0,2},{1,3},{2,0},{3,1},{4,6},{5,7},{6,4},{7,5},{8,10},{9,11},{10,... | collective-permute-start | bytes 417800 | tf_op jit(solution)/shard_map/ppermute | solution.py:484
  23.3 11.1 %collective-permute-start.4 = (bf16[272,256]{1,0:T(8,128)(2,1)S(1)}, bf16[272,256]{1,0:T(8,128)(2,1)S(1)}, u32[]{:S(2)}, u32[]{:S(2)}) collective-permute-start(bf16[272,256]{1,0:T(8,128)(2,1)S(1)} %get-tuple-element.21), channel_id=1, source_target_pairs={{0,4},{1,5},{2,6},{3,7},{4,0},{5,1},{6,2},{7,3},{8,12},{9,13},{10,... | collective-permute-start | bytes 417800 | tf_op jit(solution)/shard_map/ppermute | solution.py:484
  26.5 6.7 %collective-permute-start.7 = (bf16[32,1024]{1,0:T(8,128)(2,1)S(1)}, bf16[32,1024]{1,0:T(8,128)(2,1)S(1)}, u32[]{:S(2)}, u32[]{:S(2)}) collective-permute-start(bf16[32,1024]{1,0:T(8,128)(2,1)S(1)} %copy-done), channel_id=1, source_target_pairs={{0,4},{1,5},{2,6},{3,7},{4,0},{5,1},{6,2},{7,3},{8,12},{9,13},{10,... | collective-permute-start | bytes 196616 | tf_op jit(solution)/shard_map/ppermute | solution.py:484
  33.2 5.0 %collective-permute-start.8 = (bf16[64,1024]{1,0:T(8,128)(2,1)S(1)}, bf16[64,1024]{1,0:T(8,128)(2,1)S(1)}, u32[]{:S(2)}, u32[]{:S(2)}) collective-permute-start(bf16[64,1024]{1,0:T(8,128)(2,1)S(1)} %join.5.a_ref), channel_id=1, source_target_pairs={{0,1},{1,0},{2,3},{3,2},{4,5},{5,4},{6,7},{7,6},{8,9},{9,8},{10,11... | collective-permute-start | bytes 393224 | tf_op jit(solution)/shard_map/ppermute | solution.py:484
  34.6 5.0 %collective-permute-start.5 = (bf16[256,256]{1,0:T(8,128)(2,1)S(1)}, bf16[256,256]{1,0:T(8,128)(2,1)S(1)}, u32[]{:S(2)}, u32[]{:S(2)}) collective-permute-start(bf16[256,256]{1,0:T(8,128)(2,1)S(1)} %coarse.1.a_ref), channel_id=1, source_target_pairs={{0,16},{1,17},{2,18},{3,19},{4,20},{5,21},{6,22},{7,23},{8,24},{9,... | collective-permute-start | bytes 393224 | tf_op jit(solution)/shard_map/ppermute | solution.py:484
  38.2 6.4 %collective-permute-start.9 = (bf16[128,1024]{1,0:T(8,128)(2,1)S(1)}, bf16[128,1024]{1,0:T(8,128)(2,1)S(1)}, u32[]{:S(2)}, u32[]{:S(2)}) collective-permute-start(bf16[128,1024]{1,0:T(8,128)(2,1)S(1)} %join.6), channel_id=1, source_target_pairs={{0,2},{1,3},{2,0},{3,1},{4,6},{5,7},{6,4},{7,5},{8,10},{9,11},{10,... | collective-permute-start | bytes 786440 | tf_op jit(solution)/shard_map/ppermute | solution.py:484
  39.7 5.0 %collective-permute-start.6 = (bf16[512,256]{1,0:T(8,128)(2,1)S(1)}, bf16[512,256]{1,0:T(8,128)(2,1)S(1)}, u32[]{:S(2)}, u32[]{:S(2)}) collective-permute-start(bf16[512,256]{1,0:T(8,128)(2,1)S(1)} %join.4.refs_0_), channel_id=1, source_target_pairs={{0,8},{1,9},{2,10},{3,11},{4,12},{5,13},{6,14},{7,15},{8,0},{9,1},... | collective-permute-start | bytes 786440 | tf_op jit(solution)/shard_map/ppermute | solution.py:484
  41.1 11.6 %collective-permute-start.10 = (bf16[4,128,256]{2,1,0:T(8,128)(2,1)S(1)}, bf16[4,128,256]{2,1,0:T(8,128)(2,1)S(1)}, u32[]{:S(2)}, u32[]{:S(2)}) collective-permute-start(bf16[4,128,256]{2,1,0:T(8,128)(2,1)S(1)} %get-tuple-element.17), channel_id=1, source_target_pairs={{0,8},{8,16},{16,24},{24,0},{1,9},{9,17},{17,25},{25,1},{2,10},{10... | collective-permute-start | bytes 786440 | tf_op jit(solution)/shard_map/ppermute | solution.py:515
  41.6 11.1 %collective-permute-start.11 = (bf16[4,128,256]{2,1,0:T(8,128)(2,1)S(1)}, bf16[4,128,256]{2,1,0:T(8,128)(2,1)S(1)}, u32[]{:S(2)}, u32[]{:S(2)}) collective-permute-start(bf16[4,128,256]{2,1,0:T(8,128)(2,1)S(1)} %get-tuple-element.18), channel_id=1, source_target_pairs={{8,0},{16,8},{24,16},{0,24},{9,1},{17,9},{25,17},{1,25},{10,2},{18... | collective-permute-start | bytes 786440 | tf_op jit(solution)/shard_map/ppermute | solution.py:516
  45.1 7.5 %collective-permute-start.12 = (bf16[256,256]{1,0:T(8,128)(2,1)S(1)}, bf16[256,256]{1,0:T(8,128)(2,1)S(1)}, u32[]{:S(2)}, u32[]{:S(2)}) collective-permute-start(bf16[256,256]{1,0:T(8,128)(2,1)S(1)} %mix.1.m_ref.a_ref), channel_id=1, source_target_pairs={{0,16},{1,17},{2,18},{3,19},{4,20},{5,21},{6,22},{7,23},{8,24},{9,... | collective-permute-start | bytes 393224 | tf_op jit(solution)/shard_map/ppermute | solution.py:484
  52.6 7.9 %collective-permute-start.13 = (bf16[512,256]{1,0:T(8,128)(2,1)S(1)}, bf16[512,256]{1,0:T(8,128)(2,1)S(1)}, u32[]{:S(2)}, u32[]{:S(2)}) collective-permute-start(bf16[512,256]{1,0:T(8,128)(2,1)S(1)} %join.7), channel_id=1, source_target_pairs={{0,8},{1,9},{2,10},{3,11},{4,12},{5,13},{6,14},{7,15},{8,0},{9,1},... | collective-permute-start | bytes 786440 | tf_op jit(solution)/shard_map/ppermute | solution.py:484
  52.7 6.2 %copy-start.3 = (s32[4096]{0:T(1024)S(1)}, s32[4096]{0:T(1024)}, u32[]{:S(2)}) copy-start(s32[4096]{0:T(1024)} %param.17) | copy-start | bytes 49156
